TPU v7x, 32 devices: a whole 2x2x4 slice. The times are simulated.
32 devices in a mesh: groups: 2 (over y), adapter: 4 (over x, core), tensor: 4 (over z).
Axes of the slice: x: 2, y: 2, z: 4, core: 2. Of those that a mesh axis runs over, the one named last changes fastest.
Arguments:
- tokens: bfloat16 [2048, 8192], P(('groups', 'adapter'), 'tensor'), parts along dimension 0, may hold values from -6 to 6
- query_weight: bfloat16 [8192, 8192], P('tensor', 'adapter'), may hold values from -0.0625 to 0.0625
- adapter_down_weight: bfloat16 [128, 16, 8192], P('adapter', None, 'tensor'), may hold values from -0.0625 to 0.0625
- adapter_up_weight: bfloat16 [128, 16, 8192], P('adapter'), may hold values from -1.5 to 1.5
- block_adapter_ids: int32 [16], P('groups'), parts along dimension 0, may hold values from 0 to 127, as said below
- block_live_count: int32 [16], P('groups'), parts along dimension 0, may hold values from 1 to 128
- adapter_slot_index: int32 [256], P('groups'), parts along dimension 0, may hold values from 0 to 127, as said below
Outputs:
- query: bfloat16 [2048, 8192], P(('groups', 'tensor'), 'adapter'), parts along dimension 0
There are 2 independent parts, one for each index of `groups`. A program takes and returns all parts, laid end to end along the dimension named above; an argument that names none is the same for every part. Nothing has to cross between parts.
Inputs may be any that keep to these rules, and one draw needn't show every extreme that they name: Counting blocks by the owner range adapter_slot_index[block_adapter_ids[k]] // 32, no owner has more than 4 blocks, and one owner has exactly 4 in every draw. `adapter_slot_index`: A permutation: each slot holds exactly one adapter.
All inputs are finite; a program needn't handle non-finite values.
Results may differ from a plain program's by a relative error of at most 0.014.
Values may be sent and summed in bfloat16 or wider, within the bound.
A program may use at most 128 MiB of HBM per device.

v0:
```python
import functools

import jax
import jax.numpy as jnp
from jax import lax
from jax.experimental import pallas as pl
from jax.experimental.pallas import tpu as pltpu
from jax.sharding import PartitionSpec as P

BLOCK = 128
SCALE = 2.0
MESH = pl.DeviceIdType.MESH


def kernel(
    A, T,
    ids, live, slots, tok_hbm, w_hbm, dn_hbm, up_hbm, out_ref,
    tok, w, dn, up, buf_r, buf_l, acc, dn_send, dn_recv, up_send, up_recv, s_send, s_recv,
    ld_sem, w_sem, tok_ss, tok_rs, dn_ss, dn_rs, up_ss, up_rs, s_ss, s_rs,
    r_ss, r_rs, l_ss, l_rs,
):
    a = lax.axis_index("adapter")
    t = lax.axis_index("tensor")
    chips = A // 2
    x, core = a // 2, a % 2
    partner = 2 * x + 1 - core
    rows_a = tok_hbm.shape[0]
    rows = rows_a * A
    rows_d = rows // T
    per_dev = dn_hbm.shape[0]
    np_, _, cp = buf_r.shape[1:]
    cols = np_ * cp
    nb_a = rows_a // BLOCK
    nb_t = rows_d // BLOCK

    def local(src, dst, i):
        return pltpu.make_async_copy(src, dst, ld_sem.at[i])

    my_rows = tok.at[pl.ds(pl.multiple_of(a * rows_a, rows_a), rows_a)]
    tok_load = local(tok_hbm, my_rows, 0)
    dn_load = local(dn_hbm, dn, 1)
    up_load = local(up_hbm, up, 2)
    tok_load.start()
    dn_load.start()

    def w_load(p):
        c = pl.ds(pl.multiple_of(p * cp, cp), cp)
        return pltpu.make_async_copy(w_hbm.at[:, c], w.at[p], w_sem.at[p])

    for p in range(np_):
        w_load(p).start()
    up_load.start()

    barrier = pltpu.get_barrier_semaphore()
    for i in range(1, A * T):
        q = (a * T + t + i) % (A * T)
        pl.semaphore_signal(
            barrier, inc=1, device_id={"adapter": q // T, "tensor": q % T}, device_id_type=MESH
        )
    pl.semaphore_wait(barrier, A * T - 1)

    def tok_copy(owner, to, ssem):
        r = tok.at[pl.ds(pl.multiple_of(owner * rows_a, rows_a), rows_a)]
        return pltpu.make_async_remote_copy(
            r, r, tok_ss.at[ssem], tok_rs.at[owner],
            device_id={"adapter": to}, device_id_type=MESH,
        )

    tok_load.wait()
    sends = [tok_copy(a, partner, 0)]
    for i in range(1, chips):
        sends.append(tok_copy(a, 2 * ((x + i) % chips) + core, i))
    for c in sends:
        c.start()

    def slot_of(k):
        return slots[ids[k]]

    dn_load.wait()
    for i in range(A):
        for b in range(nb_a):
            dn_send[i, b] = dn[lax.rem(slot_of(i * nb_a + b), per_dev)]
    dn_recv[a] = dn_send[a]

    def dn_copy(i):
        to = (a + i) % A
        return pltpu.make_async_remote_copy(
            dn_send.at[to], dn_recv.at[a], dn_ss.at[i], dn_rs.at[i],
            device_id={"adapter": to}, device_id_type=MESH,
        )

    local_chunks = (2 * rows_a) // rows_d
    aligned = (2 * rows_a) % rows_d == 0 and local_chunks >= 2
    high = jnp.maximum((2 * (x + 1) * rows_a - 1) // rows_d, 1)
    low = jnp.minimum((2 * x * rows_a) // rows_d, T - 2)

    def order_r(j):
        v = T - j
        v = jnp.where(v <= high, v - 1, v)
        return jnp.where(j == 0, high, v)

    def order_l(j):
        v = j - 1
        v = jnp.where(v >= low, v + 1, v)
        return jnp.where(j == 0, low, v)

    pos_r = jnp.where(t == high, 0, jnp.where(t > high, T - t, T - 1 - t))
    pos_l = jnp.where(t == low, 0, jnp.where(t < low, t + 1, t))

    def base(d, p):
        return jnp.dot(
            tok[pl.ds(pl.multiple_of(d * rows_d, rows_d), rows_d), :], w[p],
            preferred_element_type=jnp.float32,
        )

    def flow(buf, ss, rs, to, j, p):
        return pltpu.make_async_remote_copy(
            buf.at[j, p], buf.at[j, p], ss.at[j, p], rs.at[j, p],
            device_id={"tensor": to}, device_id_type=MESH,
        )

    right, left = (t + 1) % T, (t + T - 1) % T

    def step(buf, ss, rs, to, d, j, p, fresh):
        @pl.when(fresh)
        def _():
            buf[j, p] = base(d, p).astype(buf.dtype)

        @pl.when(jnp.logical_not(fresh))
        def _():
            mine = base(d, p)
            flow(buf, ss, rs, to, j, p).wait_recv()
            buf[j, p] = (mine + buf[j, p].astype(jnp.float32)).astype(buf.dtype)

        flow(buf, ss, rs, to, j, p).start()

    def wait_tokens(first):
        for i in range(1, chips):
            o = 2 * ((x + i) % chips) + core
            tok_copy(o, partner, 0).wait_recv()
            tok_copy(o, partner, chips + i - 1).start()
        for i in range(1, chips):
            o = 2 * ((x + i) % chips) + 1 - core
            tok_copy(o, partner, 0).wait_recv()

    def up_copy(i):
        to = (a + i) % A
        return pltpu.make_async_remote_copy(
            up_send.at[to], up_recv.at[a], up_ss.at[i], up_rs.at[i],
            device_id={"adapter": to}, device_id_type=MESH,
        )

    def s_dest(b):
        k = a * nb_a + b
        return k // nb_t, k % nb_t

    def s_copy(i, b):
        d, kk = s_dest(b)
        return pltpu.make_async_remote_copy(
            s_send.at[b], s_recv.at[t, kk], s_ss.at[i, b], s_rs.at[t, kk],
            device_id={"adapter": (a + i) % A, "tensor": d}, device_id_type=MESH,
        )

    def send_adapters():
        up_load.wait()
        for b in range(nb_t):
            sl = lax.rem(slot_of(t * nb_t + b), per_dev)
            for i in range(A):
                up_send[i, b] = up[sl, :, i * cols:(i + 1) * cols]
        up_recv[a] = up_send[a]
        for i in range(1, A):
            up_copy(i).start()

    def send_shrunk():
        for i in range(1, A):
            dn_copy(i).wait_recv()
        for b in range(nb_a):
            k = a * nb_a + b
            mine = dn_recv[lax.div(slot_of(k), per_dev), b]
            rows_b = tok[pl.ds(pl.multiple_of(k * BLOCK, BLOCK), BLOCK), :]
            s = lax.dot_general(
                mine, rows_b, (((1,), (1,)), ((), ())), preferred_element_type=jnp.float32
            )
            keep = lax.broadcasted_iota(jnp.int32, s.shape, 1) < live[k]
            s_send[b] = jnp.where(keep, s, 0.0).astype(s_send.dtype)
            d, kk = s_dest(b)
            for i in range(A):
                if i:
                    s_copy(i, b).start()
                else:
                    @pl.when(d == t)
                    def _():
                        s_recv[t, kk] = s_send[b]

                    @pl.when(d != t)
                    def _():
                        s_copy(0, b).start()

    def wait_adapters():
        for i in range(1, A):
            up_copy(i).wait_recv()
        for b in range(nb_t):
            owner = (t * nb_t + b) // nb_a
            for tt in range(T):
                c = pltpu.make_async_remote_copy(
                    s_send.at[0], s_recv.at[tt, b], s_ss.at[0, 0], s_rs.at[tt, b],
                    device_id={"adapter": partner}, device_id_type=MESH,
                )

                @pl.when(jnp.logical_or(owner != a, t != tt))
                def _():
                    c.wait_recv()

    def add_adapters(p):
        for b in range(nb_t):
            own = lax.div(slot_of(t * nb_t + b), per_dev)
            u = up_recv[own, b, :, pl.ds(pl.multiple_of(p * cp, cp), cp)]
            lhs = s_recv[:, b].reshape(T * s_recv.shape[2], BLOCK)
            r = slice(b * BLOCK, (b + 1) * BLOCK)
            acc[p, r] = acc[p, r] + SCALE * lax.dot_general(
                lhs, jnp.concatenate([u] * T, axis=0), (((0,), (0,)), ((), ())),
                preferred_element_type=jnp.float32,
            )

    if not aligned:
        tok_copy(partner, partner, 0).wait_recv()
        wait_tokens(True)

    for j in range(T - 1):
        if j == 0 and aligned:
            tok_copy(partner, partner, 0).wait_recv()
        if j == min(1, T - 2):
            if aligned:
                wait_tokens(True)
            for i in range(1, A):
                dn_copy(i).start()
            send_adapters()
        if j == T - 2:
            send_shrunk()
        d_r, d_l = order_r(j), order_l(j)

        def body(p, _):
            if j == 0:
                w_load(p).wait()

            @pl.when(d_r > t)
            def _():
                step(buf_r, r_ss, r_rs, right, d_r, j, p, t == 0)

            @pl.when(d_l < t)
            def _():
                step(buf_l, l_ss, l_rs, left, d_l, j, p, t == T - 1)

            if j == min(1, T - 2):
                acc[p] = base(t, p)
            return 0

        lax.fori_loop(0, np_, body, 0)

    wait_adapters()

    def last(p, _):
        add_adapters(p)

        @pl.when(t > 0)
        def _():
            flow(buf_r, r_ss, r_rs, right, pos_r, p).wait_recv()
            acc[p] = acc[p] + buf_r[pos_r, p].astype(jnp.float32)

        @pl.when(t < T - 1)
        def _():
            flow(buf_l, l_ss, l_rs, left, pos_l, p).wait_recv()
            acc[p] = acc[p] + buf_l[pos_l, p].astype(jnp.float32)

        out_ref[:, pl.ds(pl.multiple_of(p * cp, cp), cp)] = acc[p].astype(out_ref.dtype)
        return 0

    lax.fori_loop(0, np_, last, 0)

    for c in sends:
        c.wait_send()
    for i in range(1, chips):
        tok_copy(a, partner, chips + i - 1).wait_send()
    for i in range(1, A):
        dn_copy(i).wait_send()
        up_copy(i).wait_send()
    for b in range(nb_a):
        d, _ = s_dest(b)
        for i in range(1, A):
            s_copy(i, b).wait_send()

        @pl.when(d != t)
        def _():
            s_copy(0, b).wait_send()
    for j in range(T - 1):
        d_r, d_l = order_r(j), order_l(j)

        def drain(p, _):
            @pl.when(d_r > t)
            def _():
                flow(buf_r, r_ss, r_rs, right, j, p).wait_send()

            @pl.when(d_l < t)
            def _():
                flow(buf_l, l_ss, l_rs, left, j, p).wait_send()
            return 0

        lax.fori_loop(0, np_, drain, 0)


def on_device(tokens, query_weight, down, up, ids, live, slots):
    A, T = lax.axis_size("adapter"), lax.axis_size("tensor")
    rows_a, feat = tokens.shape
    cols = query_weight.shape[1]
    rank = down.shape[1]
    rows_d = rows_a * A // T
    cp = min(256, cols)
    np_ = cols // cp
    nb_a, nb_t = rows_a // BLOCK, rows_d // BLOCK
    chips = A // 2
    bf, f32 = jnp.bfloat16, jnp.float32
    dma = pltpu.SemaphoreType.DMA
    smem = pl.BlockSpec(memory_space=pltpu.SMEM)
    hbm = pl.BlockSpec(memory_space=pl.ANY)
    return pl.pallas_call(
        functools.partial(kernel, A, T),
        out_shape=jax.ShapeDtypeStruct((rows_d, cols), bf),
        in_specs=[smem, smem, smem, hbm, hbm, hbm, hbm],
        out_specs=pl.BlockSpec(memory_space=pltpu.VMEM),
        scratch_shapes=[
            pltpu.VMEM((rows_a * A, feat), bf),
            pltpu.VMEM((np_, feat, cp), bf),
            pltpu.VMEM(down.shape, bf),
            pltpu.VMEM(up.shape, bf),
            pltpu.VMEM((T - 1, np_, rows_d, cp), bf),
            pltpu.VMEM((T - 1, np_, rows_d, cp), bf),
            pltpu.VMEM((np_, rows_d, cp), f32),
            pltpu.VMEM((A, nb_a, rank, feat), bf),
            pltpu.VMEM((A, nb_a, rank, feat), bf),
            pltpu.VMEM((A, nb_t, rank, cols), bf),
            pltpu.VMEM((A, nb_t, rank, cols), bf),
            pltpu.VMEM((nb_a, rank, BLOCK), bf),
            pltpu.VMEM((T, nb_t, rank, BLOCK), bf),
            dma((3,)), dma((np_,)),
            dma((2 * chips,)), dma((A,)),
            dma((A,)), dma((A,)), dma((A,)), dma((A,)),
            dma((A, nb_a)), dma((T, nb_t)),
            dma((T - 1, np_)), dma((T - 1, np_)), dma((T - 1, np_)), dma((T - 1, np_)),
        ],
        compiler_params=pltpu.CompilerParams(
            collective_id=0, has_side_effects=True, vmem_limit_bytes=60 * 1024 * 1024
        ),
    )(ids, live, slots, tokens, query_weight, down, up)


def solution(mesh):
    placed = (
        P(("groups", "adapter"), "tensor"),
        P("tensor", "adapter"),
        P("adapter", None, "tensor"),
        P("adapter", None, None),
        P("groups"),
        P("groups"),
        P("groups"),
    )
    return jax.shard_map(
        on_device,
        mesh=mesh,
        in_specs=placed,
        out_specs=P(("groups", "tensor"), "adapter"),
        check_vma=False,
    )
```

profile of v0, /device:TPU:16, one launch (start us, length us, event | category | flops | bytes accessed | tf_op | source)
XLA Modules:
  0.0 92.1 jit_solution(8148199423641758958)
XLA Ops:
  0.0 89.8 %shard_map.73 = bf16[256,2048]{1,0:T(8,128)(2,1)} custom-call(s32[8]{0:T(128)} %ids.1, s32[8]{0:T(128)} %live.1, s32[128]{0:T(128)} %slots.1, bf16[256,2048]{1,0:T(8,128)(2,1)} %tok_hbm.1, bf16[2048,2048]{1,0:T(8,128)(2,1)} %w_hbm.1, bf16[32,16,2048]{2,1,0:T(8,128)(2,1)} %dn_hbm.1, bf16[32,16,8192]{2,1,0:T(8,128)(2,1)} %up_hbm.1), custom_call_target="tpu_custom_call" | custom-call | tf_op jit(solution)/shard_map/pallas_call | solution.py:325
  89.8 2.3 %copy.9 = bf16[256,2048]{1,0:T(8,128)(2,1)} copy(bf16[256,2048]{1,0:T(8,128)(2,1)} %shard_map.73) | data formatting | bytes 2097152
where the time goes:
time: 92.5 us; the launch traced here: 92.1 us
  Pallas kernels  89.8 us (97%)
  local copies, waits for them, and re-layouts  2.3 us (2%)
    pallas_call x1, Pallas kernels, on_device(): pl.pallas_call(functools.partial(kernel, A, T), out_shape=jax.ShapeDtypeS...  89.8 us
    unnamed x1, local copies, waits for them, and re-layouts  2.3 us

commit v1 on v0

v1 whole, which is shorter than its diff:
```python
import functools

import jax
import jax.numpy as jnp
from jax import lax
from jax.experimental import pallas as pl
from jax.experimental.pallas import tpu as pltpu
from jax.sharding import PartitionSpec as P

BLOCK = 128
SCALE = 2.0
MESH = pl.DeviceIdType.MESH
PRE = 2


def kernel(
    A, T,
    ids, live, slots, tok_hbm, w_hbm, dn_hbm, up_hbm, out_ref,
    tok, w, dn, up, buf, acc, dn_send, dn_recv, up_send, up_recv, s_send, s_recv,
    tok_sem, ld_sem, w_sem, par_ss, par_rs, x_ss, x_rs, f_ss, f_rs,
    dn_ss, dn_rs, up_ss, up_rs, s_ss, s_rs, fl_ss, fl_rs, ready,
):
    a = lax.axis_index("adapter")
    t = lax.axis_index("tensor")
    chips = A // 2
    x, core = a // 2, a % 2
    partner = 2 * x + 1 - core
    nb = tok.shape[0]
    nb_a, nb_t = nb // A, nb // T
    half = BLOCK // 2
    per_dev = dn_hbm.shape[0]
    np_, _, cp = w.shape
    cols = np_ * cp
    steps = (T - 1) * nb_t
    near = chips == 2 and nb_a == nb_t
    pre_n = min(PRE, np_) if near else 0

    def tok_load(b):
        return pltpu.make_async_copy(
            tok_hbm.at[pl.ds(b * BLOCK, BLOCK)], tok.at[a * nb_a + b], tok_sem.at[b]
        )

    def w_load(p):
        c = pl.ds(pl.multiple_of(p * cp, cp), cp)
        return pltpu.make_async_copy(w_hbm.at[:, c], w.at[p], w_sem.at[p])

    dn_load = pltpu.make_async_copy(dn_hbm, dn, ld_sem.at[0])
    up_load = pltpu.make_async_copy(up_hbm, up, ld_sem.at[1])

    tok_load(0).start()
    w_load(0).start()
    for b in range(1, nb_a):
        tok_load(b).start()
    for p in range(1, np_):
        w_load(p).start()
    dn_load.start()
    up_load.start()

    barrier = pltpu.get_barrier_semaphore()

    def greet(**to):
        pl.semaphore_signal(barrier, inc=1, device_id=to, device_id_type=MESH)

    @pl.when(t > 0)
    def _():
        greet(tensor=t - 1)

    @pl.when(t < T - 1)
    def _():
        greet(tensor=t + 1)

    for i in range(1, A):
        greet(adapter=(a + i) % A)

    if near:
        lead_r = jnp.where(a >= 1, a, 1)
        lead_l = jnp.where(a <= T - 2, a, T - 2)
        first_r = (T - 1 - lead_r) * nb_t
        first_l = lead_l * nb_t
        pre = jnp.logical_or(
            jnp.logical_and(t == 0, a >= 1), jnp.logical_and(t == T - 1, a <= T - 2)
        )
    else:
        first_r = first_l = 0

    def place(way, k):
        first = first_l if way else first_r
        m = jnp.where(k - 1 < first, k - 1, k)
        m = jnp.where(k == 0, first, m)
        d = m // nb_t
        return (d if way else T - 1 - d), m % nb_t

    def flow(way, to, slot, h, p):
        return pltpu.make_async_remote_copy(
            buf.at[way, slot, h, p], buf.at[way, slot, h, p],
            fl_ss.at[way, slot, h, p], fl_rs.at[way, slot, h, p],
            device_id={"tensor": to}, device_id_type=MESH,
        )

    right, left = (t + 1) % T, (t + T - 1) % T

    def toward(way, slot, h, p):
        return flow(way, left if way else right, slot, h, p)

    def base(q, p):
        return jnp.dot(tok[q], w[p], preferred_element_type=jnp.float32)

    if near:
        pre_way = jnp.where(t == 0, 0, 1)
        pre_slot = jnp.where(t == 0, jnp.maximum(a - 1, 0), jnp.minimum(a, T - 2))
        pre_to = jnp.where(t == 0, 1, T - 2)

    tok_load(0).wait()
    if pre_n:

        @pl.when(pre)
        def _():
            def one(p, _):
                w_load(p).wait()
                buf[pre_way, pre_slot, 0, p] = base(a * nb_a, p).astype(buf.dtype)
                return 0

            lax.fori_loop(0, pre_n, one, 0)

    for b in range(1, nb_a):
        tok_load(b).wait()

    ends = jnp.where(t > 0, 1, 0) + jnp.where(t < T - 1, 1, 0)
    pl.semaphore_wait(barrier, A - 1 + ends)

    if pre_n:

        @pl.when(pre)
        def _():
            for p in range(pre_n):
                flow(pre_way, pre_to, pre_slot, 0, p).start()

    def par_copy(b):
        r = tok.at[a * nb_a + b]
        return pltpu.make_async_remote_copy(
            r, r, par_ss.at[b], par_rs.at[b], device_id={"adapter": partner}, device_id_type=MESH
        )

    def lead_core(c):
        return jnp.where(2 * c >= chips, 1, 0)

    def row_block(c, m):
        k = jnp.where(m < nb_a, lead_core(c), 1 - lead_core(c))
        return (2 * c + k) * nb_a + m % nb_a, k

    def part(q, k):
        return tok.at[q, pl.ds(pl.multiple_of(k * half, half), half)]

    def x_copy(i, m):
        r = part(row_block(x, m)[0], core)
        return pltpu.make_async_remote_copy(
            r, r, x_ss.at[i, m], x_rs.at[x, m],
            device_id={"adapter": 2 * ((x + i) % chips) + core}, device_id_type=MESH,
        )

    def x_arrival(c, m):
        r = part(row_block(c, m)[0], core)
        return pltpu.make_async_remote_copy(
            r, r, x_ss.at[0, m], x_rs.at[c, m],
            device_id={"adapter": partner}, device_id_type=MESH,
        )

    def pass_on(c, m):
        r = part(row_block(c, m)[0], core)
        return pltpu.make_async_remote_copy(
            r, r, f_ss.at[c, m], f_rs.at[c, m],
            device_id={"adapter": partner}, device_id_type=MESH,
        )

    for b in range(nb_a):
        par_copy(b).start()
    for m in range(2 * nb_a):

        @pl.when(row_block(x, m)[1] != core)
        def _():
            par_copy(m % nb_a).wait_recv()

        for i in range(1, chips):
            x_copy(i, m).start()

    def fetch(c, m):
        x_arrival(c, m).wait_recv()
        pass_on(c, m).start()

    def fetched(c, m):
        pass_on(c, m).wait_recv()

    def tell(i, to):
        pl.semaphore_signal(ready.at[i], inc=1, device_id={"tensor": to}, device_id_type=MESH)

    @pl.when(t == 0)
    def _():
        tell(0, right)

    @pl.when(t == T - 1)
    def _():
        tell(1, left)

    def relay():
        @pl.when(jnp.logical_and(t > 0, t < T - 1))
        def _():
            pl.semaphore_wait(ready.at[0], 1)
            tell(0, right)
            pl.semaphore_wait(ready.at[1], 1)
            tell(1, left)

    def all_in():
        @pl.when(t == 0)
        def _():
            pl.semaphore_wait(ready.at[1], 1)

        @pl.when(t == T - 1)
        def _():
            pl.semaphore_wait(ready.at[0], 1)

    def slot_of(k):
        return slots[ids[k]]

    def dn_copy(i):
        to = (a + i) % A
        return pltpu.make_async_remote_copy(
            dn_send.at[to], dn_recv.at[a], dn_ss.at[i], dn_rs.at[i],
            device_id={"adapter": to}, device_id_type=MESH,
        )

    def up_copy(i):
        to = (a + i) % A
        return pltpu.make_async_remote_copy(
            up_send.at[to], up_recv.at[a], up_ss.at[i], up_rs.at[i],
            device_id={"adapter": to}, device_id_type=MESH,
        )

    def s_dest(b):
        k = a * nb_a + b
        return k // nb_t, k % nb_t

    def s_copy(i, b):
        d, kk = s_dest(b)
        return pltpu.make_async_remote_copy(
            s_send.at[b], s_recv.at[t, kk], s_ss.at[i, b], s_rs.at[t, kk],
            device_id={"adapter": (a + i) % A, "tensor": d}, device_id_type=MESH,
        )

    def send_adapters():
        dn_load.wait()
        for i in range(A):
            for b in range(nb_a):
                dn_send[i, b] = dn[lax.rem(slot_of(i * nb_a + b), per_dev)]
        dn_recv[a] = dn_send[a]
        for i in range(1, A):
            dn_copy(i).start()
        up_load.wait()
        for b in range(nb_t):
            sl = lax.rem(slot_of(t * nb_t + b), per_dev)
            for i in range(A):
                up_send[i, b] = up[sl, :, i * cols:(i + 1) * cols]
        up_recv[a] = up_send[a]
        for i in range(1, A):
            up_copy(i).start()

    def send_shrunk():
        all_in()
        for i in range(1, A):
            dn_copy(i).wait_recv()
        for b in range(nb_a):
            k = a * nb_a + b
            mine = dn_recv[lax.div(slot_of(k), per_dev), b]
            s = lax.dot_general(
                mine, tok[k], (((1,), (1,)), ((), ())), preferred_element_type=jnp.float32
            )
            keep = lax.broadcasted_iota(jnp.int32, s.shape, 1) < live[k]
            s_send[b] = jnp.where(keep, s, 0.0).astype(s_send.dtype)
            d, kk = s_dest(b)
            for i in range(A):
                if i:
                    s_copy(i, b).start()
                else:
                    @pl.when(d == t)
                    def _():
                        s_recv[t, kk] = s_send[b]

                    @pl.when(d != t)
                    def _():
                        s_copy(0, b).start()

    def wait_adapters():
        for i in range(1, A):
            up_copy(i).wait_recv()
        for b in range(nb_t):
            owner = (t * nb_t + b) // nb_a
            for tt in range(T):
                c = pltpu.make_async_remote_copy(
                    s_send.at[0], s_recv.at[tt, b], s_ss.at[0, 0], s_rs.at[tt, b],
                    device_id={"adapter": partner}, device_id_type=MESH,
                )

                @pl.when(jnp.logical_or(owner != a, t != tt))
                def _():
                    c.wait_recv()

    remote = [(i, m) for i in range(1, chips) for m in range(2 * nb_a)]
    if not near:
        for i, m in remote:
            fetch((x + i) % chips, m)
        for i, m in remote:
            fetched((x + i) % chips, m)

    def advance(way, k, p):
        d, h = place(way, k)
        slot = d if way else d - 1
        q = d * nb_t + h
        go = (d < t) if way else (d > t)
        if pre_n:
            done = jnp.logical_and(jnp.logical_and(pre, k == 0), p < pre_n)
            go = jnp.logical_and(go, jnp.logical_not(done))

        @pl.when(go)
        def _():
            mine = base(q, p)
            fresh = (t == T - 1) if way else (t == 0)

            @pl.when(fresh)
            def _():
                buf[way, slot, h, p] = mine.astype(buf.dtype)

            @pl.when(jnp.logical_not(fresh))
            def _():
                toward(way, slot, h, p).wait_recv()
                buf[way, slot, h, p] = (
                    mine + buf[way, slot, h, p].astype(jnp.float32)
                ).astype(buf.dtype)

            toward(way, slot, h, p).start()

    def step(k, _):
        if near:

            @pl.when(jnp.logical_and(k >= 1, k <= 2 * nb_a))
            def _():
                fetch(1 - x, k - 1)
                fetched(1 - x, k - 1)

        @pl.when(k == min(1, steps - 1))
        def _():
            relay()

        @pl.when(k == min(2, steps - 1))
        def _():
            send_adapters()

        @pl.when(k == max(steps - 2, 0))
        def _():
            send_shrunk()

        def panel(p, _):
            loaded = k == 0
            if pre_n:
                loaded = jnp.logical_and(
                    loaded, jnp.logical_not(jnp.logical_and(pre, p < pre_n))
                )

            @pl.when(loaded)
            def _():
                w_load(p).wait()

            advance(0, k, p)
            advance(1, k, p)
            h = k - (steps - nb_t)

            @pl.when(h >= 0)
            def _():
                acc[h, p] = base(t * nb_t + h, p)

            return 0

        lax.fori_loop(0, np_, panel, 0)
        return 0

    lax.fori_loop(0, steps, step, 0)
    wait_adapters()

    def last(n, _):
        h, p = n // np_, n % np_
        own = lax.div(slot_of(t * nb_t + h), per_dev)
        u = up_recv[own, h, :, pl.ds(pl.multiple_of(p * cp, cp), cp)]
        lhs = s_recv[:, h].reshape(T * s_recv.shape[2], BLOCK)
        acc[h, p] = acc[h, p] + SCALE * lax.dot_general(
            lhs, jnp.concatenate([u] * T, axis=0), (((0,), (0,)), ((), ())),
            preferred_element_type=jnp.float32,
        )

        @pl.when(t > 0)
        def _():
            slot = jnp.maximum(t - 1, 0)
            toward(0, slot, h, p).wait_recv()
            acc[h, p] = acc[h, p] + buf[0, slot, h, p].astype(jnp.float32)

        @pl.when(t < T - 1)
        def _():
            slot = jnp.minimum(t, T - 2)
            toward(1, slot, h, p).wait_recv()
            acc[h, p] = acc[h, p] + buf[1, slot, h, p].astype(jnp.float32)

        out_ref[
            pl.ds(pl.multiple_of(h * BLOCK, BLOCK), BLOCK), pl.ds(pl.multiple_of(p * cp, cp), cp)
        ] = acc[h, p].astype(out_ref.dtype)
        return 0

    lax.fori_loop(0, nb_t * np_, last, 0)

    for b in range(nb_a):
        par_copy(b).wait_send()
    for i, m in remote:
        x_copy(i, m).wait_send()
        pass_on((x + i) % chips, m).wait_send()
    for i in range(1, A):
        dn_copy(i).wait_send()
        up_copy(i).wait_send()
    for b in range(nb_a):
        d, _ = s_dest(b)
        for i in range(1, A):
            s_copy(i, b).wait_send()

        @pl.when(d != t)
        def _():
            s_copy(0, b).wait_send()

    def drain(n, _):
        k, p = n // np_, n % np_
        for way in range(2):
            d, h = place(way, k)
            slot = d if way else d - 1

            @pl.when((d < t) if way else (d > t))
            def _():
                toward(way, slot, h, p).wait_send()

        return 0

    lax.fori_loop(0, steps * np_, drain, 0)


def on_device(tokens, query_weight, down, up, ids, live, slots):
    A, T = lax.axis_size("adapter"), lax.axis_size("tensor")
    rows_a, feat = tokens.shape
    cols = query_weight.shape[1]
    rank = down.shape[1]
    rows_d = rows_a * A // T
    cp = min(512, cols)
    np_ = cols // cp
    nb_a, nb_t = rows_a // BLOCK, rows_d // BLOCK
    chips = A // 2
    bf, f32 = jnp.bfloat16, jnp.float32
    dma = pltpu.SemaphoreType.DMA
    smem = pl.BlockSpec(memory_space=pltpu.SMEM)
    hbm = pl.BlockSpec(memory_space=pl.ANY)
    return pl.pallas_call(
        functools.partial(kernel, A, T),
        out_shape=jax.ShapeDtypeStruct((rows_d, cols), bf),
        in_specs=[smem, smem, smem, hbm, hbm, hbm, hbm],
        out_specs=pl.BlockSpec(memory_space=pltpu.VMEM),
        scratch_shapes=[
            pltpu.VMEM((A * nb_a, BLOCK, feat), bf),
            pltpu.VMEM((np_, feat, cp), bf),
            pltpu.VMEM(down.shape, bf),
            pltpu.VMEM(up.shape, bf),
            pltpu.VMEM((2, T - 1, nb_t, np_, BLOCK, cp), bf),
            pltpu.VMEM((nb_t, np_, BLOCK, cp), f32),
            pltpu.VMEM((A, nb_a, rank, feat), bf),
            pltpu.VMEM((A, nb_a, rank, feat), bf),
            pltpu.VMEM((A, nb_t, rank, cols), bf),
            pltpu.VMEM((A, nb_t, rank, cols), bf),
            pltpu.VMEM((nb_a, rank, BLOCK), bf),
            pltpu.VMEM((T, nb_t, rank, BLOCK), bf),
            dma((nb_a,)), dma((2,)), dma((np_,)),
            dma((nb_a,)), dma((nb_a,)),
            dma((chips, 2 * nb_a)), dma((chips, 2 * nb_a)),
            dma((chips, 2 * nb_a)), dma((chips, 2 * nb_a)),
            dma((A,)), dma((A,)), dma((A,)), dma((A,)),
            dma((A, nb_a)), dma((T, nb_t)),
            dma((2, T - 1, nb_t, np_)), dma((2, T - 1, nb_t, np_)),
            pltpu.SemaphoreType.REGULAR((2,)),
        ],
        compiler_params=pltpu.CompilerParams(
            collective_id=0, has_side_effects=True, vmem_limit_bytes=60 * 1024 * 1024
        ),
    )(ids, live, slots, tokens, query_weight, down, up)


def solution(mesh):
    placed = (
        P(("groups", "adapter"), "tensor"),
        P("tensor", "adapter"),
        P("adapter", None, "tensor"),
        P("adapter", None, None),
        P("groups"),
        P("groups"),
        P("groups"),
    )
    return jax.shard_map(
        on_device,
        mesh=mesh,
        in_specs=placed,
        out_specs=P(("groups", "tensor"), "adapter"),
        check_vma=False,
    )
```

time: 92.5 us -> 129 us (1.39)
  Pallas kernels: 89.8 us -> 126 us
    pallas_call x1, Pallas kernels: 89.8 us -> 126 us  [on_device(): pl.pallas_call(functools.partial(kernel, A, T), out_shape=jax.ShapeDtypeS...]
where the time goes in v1:
time: 129 us
  Pallas kernels  126 us (98%)
  local copies, waits for them, and re-layouts  2.3 us (2%)
    pallas_call x1, Pallas kernels, on_device(): pl.pallas_call(functools.partial(kernel, A, T), out_shape=jax.ShapeDtypeS...  126 us

profile of v1, /device:TPU:16, one launch (start us, length us, event | category | flops | bytes accessed | tf_op | source)
XLA Modules:
  0.0 128.5 jit_solution(6191579923695893993)
XLA Ops:
  0.0 126.2 %shard_map.73 = bf16[256,2048]{1,0:T(8,128)(2,1)} custom-call(s32[8]{0:T(128)} %ids.1, s32[8]{0:T(128)} %live.1, s32[128]{0:T(128)} %slots.1, bf16[256,2048]{1,0:T(8,128)(2,1)} %tok_hbm.1, bf16[2048,2048]{1,0:T(8,128)(2,1)} %w_hbm.1, bf16[32,16,2048]{2,1,0:T(8,128)(2,1)} %dn_hbm.1, bf16[32,16,8192]{2,1,0:T(8,128)(2,1)} %up_hbm.1), custom_call_target="tpu_custom_call" | custom-call | tf_op jit(solution)/shard_map/pallas_call | solution.py:462
  126.2 2.3 %copy.9 = bf16[256,2048]{1,0:T(8,128)(2,1)} copy(bf16[256,2048]{1,0:T(8,128)(2,1)} %shard_map.73) | data formatting | bytes 2097152

commit v2 on v1

--- a/solution.py
+++ b/solution.py
@@ -11,6 +11,7 @@
 SCALE = 2.0
 MESH = pl.DeviceIdType.MESH
 PRE = 2
+LAG = 3
 
 
 def kernel(
@@ -310,18 +311,23 @@
         for i, m in remote:
             fetched((x + i) % chips, m)
 
-    def advance(way, k, p):
+    units = steps * np_
+    lags = (LAG * t, LAG * (T - 1 - t))
+
+    def advance(way, n):
+        m = n - lags[way]
+        inside = jnp.logical_and(m >= 0, m < units)
+        m = jnp.clip(m, 0, units - 1)
+        k, p = m // np_, m % np_
         d, h = place(way, k)
         slot = d if way else d - 1
-        q = d * nb_t + h
-        go = (d < t) if way else (d > t)
+        go = jnp.logical_and(inside, (d < t) if way else (d > t))
         if pre_n:
-            done = jnp.logical_and(jnp.logical_and(pre, k == 0), p < pre_n)
-            go = jnp.logical_and(go, jnp.logical_not(done))
+            go = jnp.logical_and(go, jnp.logical_not(jnp.logical_and(pre, m < pre_n)))
 
         @pl.when(go)
         def _():
-            mine = base(q, p)
+            mine = base(d * nb_t + h, p)
             fresh = (t == T - 1) if way else (t == 0)
 
             @pl.when(fresh)
@@ -337,51 +343,48 @@
 
             toward(way, slot, h, p).start()
 
-    def step(k, _):
+    def iteration(n, _):
+        k, p = n // np_, n % np_
         if near:
 
-            @pl.when(jnp.logical_and(k >= 1, k <= 2 * nb_a))
+            @pl.when(jnp.logical_and(p == 0, jnp.logical_and(k >= 1, k <= 2 * nb_a)))
             def _():
                 fetch(1 - x, k - 1)
                 fetched(1 - x, k - 1)
 
-        @pl.when(k == min(1, steps - 1))
+        @pl.when(n == min(1, steps - 1) * np_)
         def _():
             relay()
 
-        @pl.when(k == min(2, steps - 1))
+        @pl.when(n == min(2, steps - 1) * np_)
         def _():
             send_adapters()
 
-        @pl.when(k == max(steps - 2, 0))
+        @pl.when(n == max(steps - 2, 0) * np_)
         def _():
             send_shrunk()
 
-        def panel(p, _):
-            loaded = k == 0
-            if pre_n:
-                loaded = jnp.logical_and(
-                    loaded, jnp.logical_not(jnp.logical_and(pre, p < pre_n))
-                )
-
-            @pl.when(loaded)
-            def _():
-                w_load(p).wait()
-
-            advance(0, k, p)
-            advance(1, k, p)
-            h = k - (steps - nb_t)
-
-            @pl.when(h >= 0)
-            def _():
-                acc[h, p] = base(t * nb_t + h, p)
-
-            return 0
-
-        lax.fori_loop(0, np_, panel, 0)
+        loaded = k == 0
+        if pre_n:
+            loaded = jnp.logical_and(
+                loaded, jnp.logical_not(jnp.logical_and(pre, p < pre_n))
+            )
+
+        @pl.when(loaded)
+        def _():
+            w_load(p).wait()
+
+        advance(0, n)
+        advance(1, n)
+        h = k - (steps - nb_t)
+
+        @pl.when(jnp.logical_and(h >= 0, h < nb_t))
+        def _():
+            acc[h, p] = base(t * nb_t + h, p)
+
         return 0
 
-    lax.fori_loop(0, steps, step, 0)
+    lax.fori_loop(0, units + LAG * (T - 2), iteration, 0)
     wait_adapters()
 
     def last(n, _):

time: 129 us -> 82 us (0.64)
  Pallas kernels: 126 us -> 79 us
    pallas_call x1, Pallas kernels: 126 us -> 79 us  [on_device(): pl.pallas_call(functools.partial(kernel, A, T), out_shape=jax.ShapeDtypeS...]
where the time goes in v2:
time: 82 us; the launch traced here: 81.3 us
  Pallas kernels  79 us (96%)
  local copies, waits for them, and re-layouts  2.3 us (3%)
    pallas_call x1, Pallas kernels, on_device(): pl.pallas_call(functools.partial(kernel, A, T), out_shape=jax.ShapeDtypeS...  79 us
    unnamed x1, local copies, waits for them, and re-layouts  2.3 us

profile of v2, /device:TPU:16, one launch (start us, length us, event | category | flops | bytes accessed | tf_op | source)
XLA Modules:
  0.0 81.3 jit_solution(5813730563631192215)
XLA Ops:
  0.0 79.0 %shard_map.73 = bf16[256,2048]{1,0:T(8,128)(2,1)} custom-call(s32[8]{0:T(128)} %ids.1, s32[8]{0:T(128)} %live.1, s32[128]{0:T(128)} %slots.1, bf16[256,2048]{1,0:T(8,128)(2,1)} %tok_hbm.1, bf16[2048,2048]{1,0:T(8,128)(2,1)} %w_hbm.1, bf16[32,16,2048]{2,1,0:T(8,128)(2,1)} %dn_hbm.1, bf16[32,16,8192]{2,1,0:T(8,128)(2,1)} %up_hbm.1), custom_call_target="tpu_custom_call" | custom-call | tf_op jit(solution)/shard_map/pallas_call | solution.py:465
  79.0 2.3 %copy.9 = bf16[256,2048]{1,0:T(8,128)(2,1)} copy(bf16[256,2048]{1,0:T(8,128)(2,1)} %shard_map.73) | data formatting | bytes 2097152

commit v3 on v2

--- a/solution.py
+++ b/solution.py
@@ -10,7 +10,7 @@
 BLOCK = 128
 SCALE = 2.0
 MESH = pl.DeviceIdType.MESH
-PRE = 2
+PRE = (2, 1)
 LAG = 3
 
 
@@ -34,7 +34,6 @@
     cols = np_ * cp
     steps = (T - 1) * nb_t
     near = chips == 2 and nb_a == nb_t
-    pre_n = min(PRE, np_) if near else 0
 
     def tok_load(b):
         return pltpu.make_async_copy(
@@ -94,7 +93,7 @@
     def flow(way, to, slot, h, p):
         return pltpu.make_async_remote_copy(
             buf.at[way, slot, h, p], buf.at[way, slot, h, p],
-            fl_ss.at[way, slot, h, p], fl_rs.at[way, slot, h, p],
+            fl_ss.at[way, slot], fl_rs.at[way, slot, h, p],
             device_id={"tensor": to}, device_id_type=MESH,
         )
 
@@ -111,30 +110,27 @@
         pre_slot = jnp.where(t == 0, jnp.maximum(a - 1, 0), jnp.minimum(a, T - 2))
         pre_to = jnp.where(t == 0, 1, T - 2)
 
+    def lead_unit(p):
+        w_load(p).wait()
+        buf[pre_way, pre_slot, 0, p] = base(a * nb_a, p).astype(buf.dtype)
+
     tok_load(0).wait()
-    if pre_n:
+    if near:
+        early = jnp.where(t == 0, min(PRE[0], np_), min(PRE[1], np_))
 
         @pl.when(pre)
         def _():
             def one(p, _):
-                w_load(p).wait()
-                buf[pre_way, pre_slot, 0, p] = base(a * nb_a, p).astype(buf.dtype)
+                lead_unit(p)
                 return 0
 
-            lax.fori_loop(0, pre_n, one, 0)
+            lax.fori_loop(0, early, one, 0)
 
     for b in range(1, nb_a):
         tok_load(b).wait()
 
     ends = jnp.where(t > 0, 1, 0) + jnp.where(t < T - 1, 1, 0)
     pl.semaphore_wait(barrier, A - 1 + ends)
-
-    if pre_n:
-
-        @pl.when(pre)
-        def _():
-            for p in range(pre_n):
-                flow(pre_way, pre_to, pre_slot, 0, p).start()
 
     def par_copy(b):
         r = tok.at[a * nb_a + b]
@@ -173,16 +169,56 @@
             device_id={"adapter": partner}, device_id_type=MESH,
         )
 
+    def send_x(m):
+        for i in range(1, chips):
+            x_copy(i, m).start()
+
+    if near:
+
+        @pl.when(pre)
+        def _():
+            def one(p, _):
+                flow(pre_way, pre_to, pre_slot, 0, p).start()
+                return 0
+
+            lax.fori_loop(0, early, one, 0)
+
     for b in range(nb_a):
         par_copy(b).start()
-    for m in range(2 * nb_a):
-
-        @pl.when(row_block(x, m)[1] != core)
-        def _():
-            par_copy(m % nb_a).wait_recv()
-
-        for i in range(1, chips):
-            x_copy(i, m).start()
+
+    own_first = lead_core(x) == core
+
+    @pl.when(own_first)
+    def _():
+        for m in range(nb_a):
+            send_x(m)
+
+    if near:
+
+        @pl.when(pre)
+        def _():
+            def one(p, _):
+                lead_unit(p)
+                flow(pre_way, pre_to, pre_slot, 0, p).start()
+                return 0
+
+            lax.fori_loop(early, np_, one, 0)
+
+    for b in range(nb_a):
+        par_copy(b).wait_recv()
+
+        @pl.when(own_first)
+        def _():
+            send_x(nb_a + b)
+
+        @pl.when(jnp.logical_not(own_first))
+        def _():
+            send_x(b)
+
+    @pl.when(jnp.logical_not(own_first))
+    def _():
+        for m in range(nb_a, 2 * nb_a):
+            send_x(m)
 
     def fetch(c, m):
         x_arrival(c, m).wait_recv()
@@ -322,8 +358,8 @@
         d, h = place(way, k)
         slot = d if way else d - 1
         go = jnp.logical_and(inside, (d < t) if way else (d > t))
-        if pre_n:
-            go = jnp.logical_and(go, jnp.logical_not(jnp.logical_and(pre, m < pre_n)))
+        if near:
+            go = jnp.logical_and(go, jnp.logical_not(jnp.logical_and(pre, m < np_)))
 
         @pl.when(go)
         def _():
@@ -365,10 +401,8 @@
             send_shrunk()
 
         loaded = k == 0
-        if pre_n:
-            loaded = jnp.logical_and(
-                loaded, jnp.logical_not(jnp.logical_and(pre, p < pre_n))
-            )
+        if near:
+            loaded = jnp.logical_and(loaded, jnp.logical_not(pre))
 
         @pl.when(loaded)
         def _():
@@ -386,36 +420,6 @@
 
     lax.fori_loop(0, units + LAG * (T - 2), iteration, 0)
     wait_adapters()
-
-    def last(n, _):
-        h, p = n // np_, n % np_
-        own = lax.div(slot_of(t * nb_t + h), per_dev)
-        u = up_recv[own, h, :, pl.ds(pl.multiple_of(p * cp, cp), cp)]
-        lhs = s_recv[:, h].reshape(T * s_recv.shape[2], BLOCK)
-        acc[h, p] = acc[h, p] + SCALE * lax.dot_general(
-            lhs, jnp.concatenate([u] * T, axis=0), (((0,), (0,)), ((), ())),
-            preferred_element_type=jnp.float32,
-        )
-
-        @pl.when(t > 0)
-        def _():
-            slot = jnp.maximum(t - 1, 0)
-            toward(0, slot, h, p).wait_recv()
-            acc[h, p] = acc[h, p] + buf[0, slot, h, p].astype(jnp.float32)
-
-        @pl.when(t < T - 1)
-        def _():
-            slot = jnp.minimum(t, T - 2)
-            toward(1, slot, h, p).wait_recv()
-            acc[h, p] = acc[h, p] + buf[1, slot, h, p].astype(jnp.float32)
-
-        out_ref[
-            pl.ds(pl.multiple_of(h * BLOCK, BLOCK), BLOCK), pl.ds(pl.multiple_of(p * cp, cp), cp)
-        ] = acc[h, p].astype(out_ref.dtype)
-        return 0
-
-    lax.fori_loop(0, nb_t * np_, last, 0)
-
     for b in range(nb_a):
         par_copy(b).wait_send()
     for i, m in remote:
@@ -433,19 +437,45 @@
         def _():
             s_copy(0, b).wait_send()
 
-    def drain(n, _):
-        k, p = n // np_, n % np_
-        for way in range(2):
-            d, h = place(way, k)
-            slot = d if way else d - 1
-
-            @pl.when((d < t) if way else (d > t))
+    def last(n, _):
+        h, p = n // np_, n % np_
+        own = lax.div(slot_of(t * nb_t + h), per_dev)
+        u = up_recv[own, h, :, pl.ds(pl.multiple_of(p * cp, cp), cp)]
+        lhs = s_recv[:, h].reshape(T * s_recv.shape[2], BLOCK)
+        acc[h, p] = acc[h, p] + SCALE * lax.dot_general(
+            lhs, jnp.concatenate([u] * T, axis=0), (((0,), (0,)), ((), ())),
+            preferred_element_type=jnp.float32,
+        )
+
+        @pl.when(t > 0)
+        def _():
+            slot = jnp.maximum(t - 1, 0)
+            toward(0, slot, h, p).wait_recv()
+            acc[h, p] = acc[h, p] + buf[0, slot, h, p].astype(jnp.float32)
+
+        @pl.when(t < T - 1)
+        def _():
+            slot = jnp.minimum(t, T - 2)
+            toward(1, slot, h, p).wait_recv()
+            acc[h, p] = acc[h, p] + buf[1, slot, h, p].astype(jnp.float32)
+
+        out_ref[
+            pl.ds(pl.multiple_of(h * BLOCK, BLOCK), BLOCK), pl.ds(pl.multiple_of(p * cp, cp), cp)
+        ] = acc[h, p].astype(out_ref.dtype)
+        return 0
+
+    lax.fori_loop(0, nb_t * np_, last, 0)
+
+    for way in range(2):
+        for slot in range(T - 1):
+
+            @pl.when((slot < t) if way else (slot + 1 > t))
             def _():
-                toward(way, slot, h, p).wait_send()
-
-        return 0
-
-    lax.fori_loop(0, steps * np_, drain, 0)
+                pltpu.make_async_remote_copy(
+                    buf.at[way, slot], buf.at[way, slot],
+                    fl_ss.at[way, slot], fl_rs.at[way, slot, 0, 0],
+                    device_id={"tensor": left if way else right}, device_id_type=MESH,
+                ).wait_send()
 
 
 def on_device(tokens, query_weight, down, up, ids, live, slots):
@@ -464,7 +494,7 @@
     hbm = pl.BlockSpec(memory_space=pl.ANY)
     return pl.pallas_call(
         functools.partial(kernel, A, T),
-        out_shape=jax.ShapeDtypeStruct((rows_d, cols), bf),
+        out_shape=pltpu.VMEM((rows_d, cols), bf),
         in_specs=[smem, smem, smem, hbm, hbm, hbm, hbm],
         out_specs=pl.BlockSpec(memory_space=pltpu.VMEM),
         scratch_shapes=[
@@ -486,7 +516,7 @@
             dma((chips, 2 * nb_a)), dma((chips, 2 * nb_a)),
             dma((A,)), dma((A,)), dma((A,)), dma((A,)),
             dma((A, nb_a)), dma((T, nb_t)),
-            dma((2, T - 1, nb_t, np_)), dma((2, T - 1, nb_t, np_)),
+            dma((2, T - 1)), dma((2, T - 1, nb_t, np_)),
             pltpu.SemaphoreType.REGULAR((2,)),
         ],
         compiler_params=pltpu.CompilerParams(

time: 82 us -> 77.9 us (0.950)
  Pallas kernels: 79 us -> 75.6 us
  local copies, waits for them, and re-layouts: 2.3 us -> 0.97 us
    pallas_call x1, Pallas kernels: 79 us -> 75.6 us  [on_device(): pl.pallas_call(functools.partial(kernel, A, T), out_shape=pltpu.VMEM((row...]
    unnamed x1, local copies, waits for them, and re-layouts: 2.3 us -> 0.97 us
where the time goes in v3:
time: 77.9 us; the launch traced here: 76.6 us
  Pallas kernels  75.6 us (97%)
  local copies, waits for them, and re-layouts  0.97 us (1%)
    pallas_call x1, Pallas kernels, on_device(): pl.pallas_call(functools.partial(kernel, A, T), out_shape=pltpu.VMEM((row...  75.6 us

profile of v3, /device:TPU:16, one launch (start us, length us, event | category | flops | bytes accessed | tf_op | source)
XLA Modules:
  0.0 76.6 jit_solution(2186046393915673285)
XLA Ops:
  0.0 75.6 %shard_map.73 = bf16[256,2048]{1,0:T(8,128)(2,1)S(1)} custom-call(s32[8]{0:T(128)} %ids.1, s32[8]{0:T(128)} %live.1, s32[128]{0:T(128)} %slots.1, bf16[256,2048]{1,0:T(8,128)(2,1)} %tok_hbm.1, bf16[2048,2048]{1,0:T(8,128)(2,1)} %w_hbm.1, bf16[32,16,2048]{2,1,0:T(8,128)(2,1)} %dn_hbm.1, bf16[32,16,8192]{2,1,0:T(8,128)(2,1)} %up_hbm.1), custom_call_target="tpu_custom_call" | custom-call | tf_op jit(solution)/shard_map/pallas_call | solution.py:495
  75.6 1.0 %copy.9 = bf16[256,2048]{1,0:T(8,128)(2,1)} copy(bf16[256,2048]{1,0:T(8,128)(2,1)S(1)} %shard_map.73) | data formatting | bytes 2097152

commit v4 on v3

--- a/solution.py
+++ b/solution.py
@@ -10,15 +10,15 @@
 BLOCK = 128
 SCALE = 2.0
 MESH = pl.DeviceIdType.MESH
-PRE = (2, 1)
+PRE = 1
 LAG = 3
 
 
 def kernel(
     A, T,
-    ids, live, slots, tok_hbm, w_hbm, dn_hbm, up_hbm, out_ref,
-    tok, w, dn, up, buf, acc, dn_send, dn_recv, up_send, up_recv, s_send, s_recv,
-    tok_sem, ld_sem, w_sem, par_ss, par_rs, x_ss, x_rs, f_ss, f_rs,
+    ids_hbm, live_hbm, slots_hbm, tok_hbm, w_hbm, dn_hbm, up_hbm, out_ref,
+    ids, live, slots, tok, w, dn, up, buf, acc, dn_send, dn_recv, up_send, up_recv, s_send, s_recv,
+    sm_sem, tok_sem, ld_sem, w_sem, par_ss, par_rs, x_ss, x_rs, f_ss, f_rs,
     dn_ss, dn_rs, up_ss, up_rs, s_ss, s_rs, fl_ss, fl_rs, ready,
 ):
     a = lax.axis_index("adapter")
@@ -49,12 +49,6 @@
 
     tok_load(0).start()
     w_load(0).start()
-    for b in range(1, nb_a):
-        tok_load(b).start()
-    for p in range(1, np_):
-        w_load(p).start()
-    dn_load.start()
-    up_load.start()
 
     barrier = pltpu.get_barrier_semaphore()
 
@@ -105,6 +99,7 @@
     def base(q, p):
         return jnp.dot(tok[q], w[p], preferred_element_type=jnp.float32)
 
+    early = min(PRE, np_)
     if near:
         pre_way = jnp.where(t == 0, 0, 1)
         pre_slot = jnp.where(t == 0, jnp.maximum(a - 1, 0), jnp.minimum(a, T - 2))
@@ -115,27 +110,28 @@
         buf[pre_way, pre_slot, 0, p] = base(a * nb_a, p).astype(buf.dtype)
 
     tok_load(0).wait()
-    if near:
-        early = jnp.where(t == 0, min(PRE[0], np_), min(PRE[1], np_))
-
+    for b in range(1, nb_a):
+        tok_load(b).start()
+    for p in range(1, min(2, np_)):
+        w_load(p).start()
+
+    if near:
         @pl.when(pre)
         def _():
-            def one(p, _):
+            for p in range(early):
                 lead_unit(p)
-                return 0
-
-            lax.fori_loop(0, early, one, 0)
-
-    for b in range(1, nb_a):
-        tok_load(b).wait()
+
+    for p in range(2, np_):
+        w_load(p).start()
 
     ends = jnp.where(t > 0, 1, 0) + jnp.where(t < T - 1, 1, 0)
     pl.semaphore_wait(barrier, A - 1 + ends)
 
-    def par_copy(b):
-        r = tok.at[a * nb_a + b]
-        return pltpu.make_async_remote_copy(
-            r, r, par_ss.at[b], par_rs.at[b], device_id={"adapter": partner}, device_id_type=MESH
+    def par_copy(b, k):
+        r = part(a * nb_a + b, k)
+        return pltpu.make_async_remote_copy(
+            r, r, par_ss.at[b, k], par_rs.at[b, k],
+            device_id={"adapter": partner}, device_id_type=MESH,
         )
 
     def lead_core(c):
@@ -177,14 +173,14 @@
 
         @pl.when(pre)
         def _():
-            def one(p, _):
+            for p in range(early):
                 flow(pre_way, pre_to, pre_slot, 0, p).start()
-                return 0
-
-            lax.fori_loop(0, early, one, 0)
 
     for b in range(nb_a):
-        par_copy(b).start()
+        if b:
+            tok_load(b).wait()
+        par_copy(b, 1 - core).start()
+        par_copy(b, core).start()
 
     own_first = lead_core(x) == core
 
@@ -193,8 +189,7 @@
         for m in range(nb_a):
             send_x(m)
 
-    if near:
-
+    def lead_units(lo, hi):
         @pl.when(pre)
         def _():
             def one(p, _):
@@ -202,10 +197,10 @@
                 flow(pre_way, pre_to, pre_slot, 0, p).start()
                 return 0
 
-            lax.fori_loop(early, np_, one, 0)
-
-    for b in range(nb_a):
-        par_copy(b).wait_recv()
+            lax.fori_loop(lo, hi, one, 0)
+
+    def from_partner(b):
+        par_copy(b, core).wait_recv()
 
         @pl.when(own_first)
         def _():
@@ -215,10 +210,32 @@
         def _():
             send_x(b)
 
-    @pl.when(jnp.logical_not(own_first))
-    def _():
-        for m in range(nb_a, 2 * nb_a):
-            send_x(m)
+        par_copy(b, 1 - core).wait_recv()
+
+    def rest_from_partner():
+        for b in range(1, nb_a):
+            from_partner(b)
+
+        @pl.when(jnp.logical_not(own_first))
+        def _():
+            for m in range(nb_a, 2 * nb_a):
+                send_x(m)
+
+    if near:
+        lead_units(early, min(early + 1, np_))
+    from_partner(0)
+    if near:
+        lead_units(min(early + 1, np_), np_)
+    dn_load.start()
+    up_load.start()
+    tables = [
+        pltpu.make_async_copy(src, dst, sm_sem.at[i])
+        for i, (src, dst) in enumerate(((ids_hbm, ids), (live_hbm, live), (slots_hbm, slots)))
+    ]
+    for c in tables:
+        c.start()
+    if not near:
+        rest_from_partner()
 
     def fetch(c, m):
         x_arrival(c, m).wait_recv()
@@ -284,6 +301,8 @@
         )
 
     def send_adapters():
+        for c in tables:
+            c.wait()
         dn_load.wait()
         for i in range(A):
             for b in range(nb_a):
@@ -348,6 +367,10 @@
             fetched((x + i) % chips, m)
 
     units = steps * np_
+    if near:
+        late = jnp.logical_or(
+            jnp.logical_and(t == 0, x == 1), jnp.logical_and(t == T - 1, x == 0)
+        )
     lags = (LAG * t, LAG * (T - 1 - t))
 
     def advance(way, n):
@@ -383,10 +406,19 @@
         k, p = n // np_, n % np_
         if near:
 
+            @pl.when(n == min(1, np_))
+            def _():
+                rest_from_partner()
+
             @pl.when(jnp.logical_and(p == 0, jnp.logical_and(k >= 1, k <= 2 * nb_a)))
             def _():
-                fetch(1 - x, k - 1)
-                fetched(1 - x, k - 1)
+                def one(m, _):
+                    fetch(1 - x, m)
+                    fetched(1 - x, m)
+                    return 0
+
+                lo = jnp.where(late, jnp.where(k == 2 * nb_a, 0, k), k - 1)
+                lax.fori_loop(lo, k, one, 0)
 
         @pl.when(n == min(1, steps - 1) * np_)
         def _():
@@ -421,7 +453,8 @@
     lax.fori_loop(0, units + LAG * (T - 2), iteration, 0)
     wait_adapters()
     for b in range(nb_a):
-        par_copy(b).wait_send()
+        par_copy(b, 0).wait_send()
+        par_copy(b, 1).wait_send()
     for i, m in remote:
         x_copy(i, m).wait_send()
         pass_on((x + i) % chips, m).wait_send()
@@ -490,14 +523,16 @@
     chips = A // 2
     bf, f32 = jnp.bfloat16, jnp.float32
     dma = pltpu.SemaphoreType.DMA
-    smem = pl.BlockSpec(memory_space=pltpu.SMEM)
     hbm = pl.BlockSpec(memory_space=pl.ANY)
     return pl.pallas_call(
         functools.partial(kernel, A, T),
         out_shape=pltpu.VMEM((rows_d, cols), bf),
-        in_specs=[smem, smem, smem, hbm, hbm, hbm, hbm],
+        in_specs=[hbm] * 7,
         out_specs=pl.BlockSpec(memory_space=pltpu.VMEM),
         scratch_shapes=[
+            pltpu.SMEM(ids.shape, ids.dtype),
+            pltpu.SMEM(live.shape, live.dtype),
+            pltpu.SMEM(slots.shape, slots.dtype),
             pltpu.VMEM((A * nb_a, BLOCK, feat), bf),
             pltpu.VMEM((np_, feat, cp), bf),
             pltpu.VMEM(down.shape, bf),
@@ -510,8 +545,8 @@
             pltpu.VMEM((A, nb_t, rank, cols), bf),
             pltpu.VMEM((nb_a, rank, BLOCK), bf),
             pltpu.VMEM((T, nb_t, rank, BLOCK), bf),
-            dma((nb_a,)), dma((2,)), dma((np_,)),
-            dma((nb_a,)), dma((nb_a,)),
+            dma((3,)), dma((nb_a,)), dma((2,)), dma((np_,)),
+            dma((nb_a, 2)), dma((nb_a, 2)),
             dma((chips, 2 * nb_a)), dma((chips, 2 * nb_a)),
             dma((chips, 2 * nb_a)), dma((chips, 2 * nb_a)),
             dma((A,)), dma((A,)), dma((A,)), dma((A,)),

time: 77.9 us -> 75.7 us (0.972)
  Pallas kernels: 75.6 us -> 73.8 us
    pallas_call x1, Pallas kernels: 75.6 us -> 73.8 us  [on_device(): pl.pallas_call(functools.partial(kernel, A, T), out_shape=pltpu.VMEM((row...]
where the time goes in v4:
time: 75.7 us; the launch traced here: 74.8 us
  Pallas kernels  73.8 us (97%)
  local copies, waits for them, and re-layouts  0.97 us (1%)
    pallas_call x1, Pallas kernels, on_device(): pl.pallas_call(functools.partial(kernel, A, T), out_shape=pltpu.VMEM((row...  73.8 us

profile of v4, /device:TPU:16, one launch (start us, length us, event | category | flops | bytes accessed | tf_op | source)
XLA Modules:
  0.0 74.8 jit_solution(15424757058078591954)
XLA Ops:
  0.0 73.8 %shard_map.73 = bf16[256,2048]{1,0:T(8,128)(2,1)S(1)} custom-call(s32[8]{0:T(128)} %ids_hbm.1, s32[8]{0:T(128)} %live_hbm.1, s32[128]{0:T(128)} %slots_hbm.1, bf16[256,2048]{1,0:T(8,128)(2,1)} %tok_hbm.1, bf16[2048,2048]{1,0:T(8,128)(2,1)} %w_hbm.1, bf16[32,16,2048]{2,1,0:T(8,128)(2,1)} %dn_hbm.1, bf16[32,16,8192]{2,1,0:T(8,128)(2,1)} %up_hbm.1), custom_call_target="tpu_custom_call" | custom-call | tf_op jit(solution)/shard_map/pallas_call | solution.py:527
  73.8 1.0 %copy.9 = bf16[256,2048]{1,0:T(8,128)(2,1)} copy(bf16[256,2048]{1,0:T(8,128)(2,1)S(1)} %shard_map.73) | data formatting | bytes 2097152

commit v5 on v4

--- a/solution.py
+++ b/solution.py
@@ -17,9 +17,10 @@
 def kernel(
     A, T,
     ids_hbm, live_hbm, slots_hbm, tok_hbm, w_hbm, dn_hbm, up_hbm, out_ref,
-    ids, live, slots, tok, w, dn, up, buf, acc, dn_send, dn_recv, up_send, up_recv, s_send, s_recv,
-    sm_sem, tok_sem, ld_sem, w_sem, par_ss, par_rs, x_ss, x_rs, f_ss, f_rs,
-    dn_ss, dn_rs, up_ss, up_rs, s_ss, s_rs, fl_ss, fl_rs, ready,
+    ids, live, slots, tok, w, dn, up, buf, acc, dn_send, dn_recv, up_send, up_recv,
+    s_send, s_col, s_recv,
+    sm_sem, ld_sem, w_sem, sent, par_rs, x_rs, f_rs, dn_rs, up_rs,
+    col_ss, col_rs, s_ss, s_rs, fl_ss, fl_rs, ready,
 ):
     a = lax.axis_index("adapter")
     t = lax.axis_index("tensor")
@@ -37,7 +38,7 @@
 
     def tok_load(b):
         return pltpu.make_async_copy(
-            tok_hbm.at[pl.ds(b * BLOCK, BLOCK)], tok.at[a * nb_a + b], tok_sem.at[b]
+            tok_hbm.at[pl.ds(b * BLOCK, BLOCK)], tok.at[a * nb_a + b], ld_sem.at[b]
         )
 
     def w_load(p):
@@ -84,10 +85,13 @@
         d = m // nb_t
         return (d if way else T - 1 - d), m % nb_t
 
+    def row(way, to, slot):
+        return jnp.where(way == 0, slot + 1, jnp.where(slot == to, T, slot))
+
     def flow(way, to, slot, h, p):
         return pltpu.make_async_remote_copy(
             buf.at[way, slot, h, p], buf.at[way, slot, h, p],
-            fl_ss.at[way, slot], fl_rs.at[way, slot, h, p],
+            fl_ss.at[way], fl_rs.at[row(way, to, slot), h, p],
             device_id={"tensor": to}, device_id_type=MESH,
         )
 
@@ -95,6 +99,13 @@
 
     def toward(way, slot, h, p):
         return flow(way, left if way else right, slot, h, p)
+
+    def arrival(way, slot, h, p):
+        return pltpu.make_async_remote_copy(
+            buf.at[way, slot, h, p], buf.at[way, slot, h, p],
+            fl_ss.at[way], fl_rs.at[row(way, t, slot), h, p],
+            device_id={"tensor": left if way else right}, device_id_type=MESH,
+        )
 
     def base(q, p):
         return jnp.dot(tok[q], w[p], preferred_element_type=jnp.float32)
@@ -130,7 +141,7 @@
     def par_copy(b, k):
         r = part(a * nb_a + b, k)
         return pltpu.make_async_remote_copy(
-            r, r, par_ss.at[b, k], par_rs.at[b, k],
+            r, r, sent.at[0], par_rs.at[b, k],
             device_id={"adapter": partner}, device_id_type=MESH,
         )
 
@@ -147,21 +158,24 @@
     def x_copy(i, m):
         r = part(row_block(x, m)[0], core)
         return pltpu.make_async_remote_copy(
-            r, r, x_ss.at[i, m], x_rs.at[x, m],
+            r, r, sent.at[1], x_rs.at[i - 1, m],
             device_id={"adapter": 2 * ((x + i) % chips) + core}, device_id_type=MESH,
         )
+
+    def hop(c):
+        return (x - c + chips) % chips - 1
 
     def x_arrival(c, m):
         r = part(row_block(c, m)[0], core)
         return pltpu.make_async_remote_copy(
-            r, r, x_ss.at[0, m], x_rs.at[c, m],
+            r, r, sent.at[1], x_rs.at[hop(c), m],
             device_id={"adapter": partner}, device_id_type=MESH,
         )
 
     def pass_on(c, m):
         r = part(row_block(c, m)[0], core)
         return pltpu.make_async_remote_copy(
-            r, r, f_ss.at[c, m], f_rs.at[c, m],
+            r, r, sent.at[2], f_rs.at[hop(c), m],
             device_id={"adapter": partner}, device_id_type=MESH,
         )
 
@@ -278,26 +292,39 @@
     def dn_copy(i):
         to = (a + i) % A
         return pltpu.make_async_remote_copy(
-            dn_send.at[to], dn_recv.at[a], dn_ss.at[i], dn_rs.at[i],
+            dn_send.at[to], dn_recv.at[a], sent.at[3], dn_rs.at[0],
             device_id={"adapter": to}, device_id_type=MESH,
         )
 
     def up_copy(i):
         to = (a + i) % A
         return pltpu.make_async_remote_copy(
-            up_send.at[to], up_recv.at[a], up_ss.at[i], up_rs.at[i],
+            up_send.at[to], up_recv.at[a], sent.at[4], up_rs.at[0],
             device_id={"adapter": to}, device_id_type=MESH,
         )
+
+    def bulk(r, i, recv):
+        return pltpu.make_async_remote_copy(
+            r, r, sent.at[i], recv, device_id={"adapter": partner}, device_id_type=MESH
+        )
+
+    dn_all = bulk(dn_recv.at[pl.ds(0, A - 1)], 3, dn_rs.at[0])
+    up_all = bulk(up_recv.at[pl.ds(0, A - 1)], 4, up_rs.at[0])
 
     def s_dest(b):
         k = a * nb_a + b
         return k // nb_t, k % nb_t
 
+    def col_copy(b):
+        return pltpu.make_async_remote_copy(
+            s_send.at[b], s_col.at[b, t], col_ss.at[b], col_rs.at[b],
+            device_id={"tensor": s_dest(b)[0]}, device_id_type=MESH,
+        )
+
     def s_copy(i, b):
-        d, kk = s_dest(b)
-        return pltpu.make_async_remote_copy(
-            s_send.at[b], s_recv.at[t, kk], s_ss.at[i, b], s_rs.at[t, kk],
-            device_id={"adapter": (a + i) % A, "tensor": d}, device_id_type=MESH,
+        return pltpu.make_async_remote_copy(
+            s_col.at[b], s_recv.at[s_dest(b)[1]], s_ss.at[b], s_rs.at[s_dest(b)[1]],
+            device_id={"adapter": (a + i) % A}, device_id_type=MESH,
         )
 
     def send_adapters():
@@ -321,8 +348,7 @@
 
     def send_shrunk():
         all_in()
-        for i in range(1, A):
-            dn_copy(i).wait_recv()
+        dn_all.wait_recv()
         for b in range(nb_a):
             k = a * nb_a + b
             mine = dn_recv[lax.div(slot_of(k), per_dev), b]
@@ -331,33 +357,41 @@
             )
             keep = lax.broadcasted_iota(jnp.int32, s.shape, 1) < live[k]
             s_send[b] = jnp.where(keep, s, 0.0).astype(s_send.dtype)
+            d, _ = s_dest(b)
+
+            @pl.when(d == t)
+            def _():
+                s_col[b, t] = s_send[b]
+
+            @pl.when(d != t)
+            def _():
+                col_copy(b).start()
+
+    def share_shrunk():
+        for b in range(nb_a):
             d, kk = s_dest(b)
-            for i in range(A):
-                if i:
+
+            @pl.when(d == t)
+            def _():
+                r = s_col.at[b, pl.ds(0, T - 1)]
+                pltpu.make_async_remote_copy(
+                    r, r, col_ss.at[b], col_rs.at[b],
+                    device_id={"tensor": right}, device_id_type=MESH,
+                ).wait_recv()
+                for i in range(1, A):
                     s_copy(i, b).start()
-                else:
-                    @pl.when(d == t)
-                    def _():
-                        s_recv[t, kk] = s_send[b]
-
-                    @pl.when(d != t)
-                    def _():
-                        s_copy(0, b).start()
+                s_recv[kk] = s_col[b]
 
     def wait_adapters():
-        for i in range(1, A):
-            up_copy(i).wait_recv()
+        up_all.wait_recv()
         for b in range(nb_t):
-            owner = (t * nb_t + b) // nb_a
-            for tt in range(T):
-                c = pltpu.make_async_remote_copy(
-                    s_send.at[0], s_recv.at[tt, b], s_ss.at[0, 0], s_rs.at[tt, b],
+
+            @pl.when((t * nb_t + b) // nb_a != a)
+            def _():
+                pltpu.make_async_remote_copy(
+                    s_recv.at[b], s_recv.at[b], s_ss.at[0], s_rs.at[b],
                     device_id={"adapter": partner}, device_id_type=MESH,
-                )
-
-                @pl.when(jnp.logical_or(owner != a, t != tt))
-                def _():
-                    c.wait_recv()
+                ).wait_recv()
 
     remote = [(i, m) for i in range(1, chips) for m in range(2 * nb_a)]
     if not near:
@@ -395,7 +429,7 @@
 
             @pl.when(jnp.logical_not(fresh))
             def _():
-                toward(way, slot, h, p).wait_recv()
+                arrival(way, slot, h, p).wait_recv()
                 buf[way, slot, h, p] = (
                     mine + buf[way, slot, h, p].astype(jnp.float32)
                 ).astype(buf.dtype)
@@ -451,30 +485,35 @@
         return 0
 
     lax.fori_loop(0, units + LAG * (T - 2), iteration, 0)
+    share_shrunk()
     wait_adapters()
-    for b in range(nb_a):
-        par_copy(b, 0).wait_send()
-        par_copy(b, 1).wait_send()
-    for i, m in remote:
-        x_copy(i, m).wait_send()
-        pass_on((x + i) % chips, m).wait_send()
-    for i in range(1, A):
-        dn_copy(i).wait_send()
-        up_copy(i).wait_send()
+    bulk(tok.at[pl.ds(0, nb_a)], 0, par_rs.at[0, 0]).wait_send()
+    if chips > 1:
+        moved = tok.at[pl.ds(0, (chips - 1) * nb_a)]
+        bulk(moved, 1, x_rs.at[0, 0]).wait_send()
+        bulk(moved, 2, f_rs.at[0, 0]).wait_send()
+    dn_all.wait_send()
+    up_all.wait_send()
     for b in range(nb_a):
         d, _ = s_dest(b)
-        for i in range(1, A):
-            s_copy(i, b).wait_send()
+
+        @pl.when(d == t)
+        def _():
+            r = dn_send.at[pl.ds(0, A - 1), 0, :, pl.ds(0, T * BLOCK)]
+            pltpu.make_async_remote_copy(
+                r, r, s_ss.at[b], s_rs.at[0],
+                device_id={"adapter": partner}, device_id_type=MESH,
+            ).wait_send()
 
         @pl.when(d != t)
         def _():
-            s_copy(0, b).wait_send()
+            col_copy(b).wait_send()
 
     def last(n, _):
         h, p = n // np_, n % np_
         own = lax.div(slot_of(t * nb_t + h), per_dev)
         u = up_recv[own, h, :, pl.ds(pl.multiple_of(p * cp, cp), cp)]
-        lhs = s_recv[:, h].reshape(T * s_recv.shape[2], BLOCK)
+        lhs = s_recv[h].reshape(T * s_recv.shape[2], BLOCK)
         acc[h, p] = acc[h, p] + SCALE * lax.dot_general(
             lhs, jnp.concatenate([u] * T, axis=0), (((0,), (0,)), ((), ())),
             preferred_element_type=jnp.float32,
@@ -483,13 +522,13 @@
         @pl.when(t > 0)
         def _():
             slot = jnp.maximum(t - 1, 0)
-            toward(0, slot, h, p).wait_recv()
+            arrival(0, slot, h, p).wait_recv()
             acc[h, p] = acc[h, p] + buf[0, slot, h, p].astype(jnp.float32)
 
         @pl.when(t < T - 1)
         def _():
             slot = jnp.minimum(t, T - 2)
-            toward(1, slot, h, p).wait_recv()
+            arrival(1, slot, h, p).wait_recv()
             acc[h, p] = acc[h, p] + buf[1, slot, h, p].astype(jnp.float32)
 
         out_ref[
@@ -499,16 +538,21 @@
 
     lax.fori_loop(0, nb_t * np_, last, 0)
 
-    for way in range(2):
-        for slot in range(T - 1):
-
-            @pl.when((slot < t) if way else (slot + 1 > t))
-            def _():
-                pltpu.make_async_remote_copy(
-                    buf.at[way, slot], buf.at[way, slot],
-                    fl_ss.at[way, slot], fl_rs.at[way, slot, 0, 0],
-                    device_id={"tensor": left if way else right}, device_id_type=MESH,
-                ).wait_send()
+    def drain(way, count):
+        r = buf.at[way, pl.ds(0, count)]
+        pltpu.make_async_remote_copy(
+            r, r, fl_ss.at[way], fl_rs.at[0, 0, 0],
+            device_id={"tensor": left if way else right}, device_id_type=MESH,
+        ).wait_send()
+
+    for i in range(T):
+
+        @pl.when(t == i)
+        def _():
+            if i < T - 1:
+                drain(0, T - 1 - i)
+            if i > 0:
+                drain(1, i)
 
 
 def on_device(tokens, query_weight, down, up, ids, live, slots):
@@ -544,14 +588,13 @@
             pltpu.VMEM((A, nb_t, rank, cols), bf),
             pltpu.VMEM((A, nb_t, rank, cols), bf),
             pltpu.VMEM((nb_a, rank, BLOCK), bf),
-            pltpu.VMEM((T, nb_t, rank, BLOCK), bf),
-            dma((3,)), dma((nb_a,)), dma((2,)), dma((np_,)),
-            dma((nb_a, 2)), dma((nb_a, 2)),
-            dma((chips, 2 * nb_a)), dma((chips, 2 * nb_a)),
-            dma((chips, 2 * nb_a)), dma((chips, 2 * nb_a)),
-            dma((A,)), dma((A,)), dma((A,)), dma((A,)),
-            dma((A, nb_a)), dma((T, nb_t)),
-            dma((2, T - 1)), dma((2, T - 1, nb_t, np_)),
+            pltpu.VMEM((nb_a, T, rank, BLOCK), bf),
+            pltpu.VMEM((nb_t, T, rank, BLOCK), bf),
+            dma((3,)), dma((max(nb_a, 2),)), dma((np_,)), dma((5,)),
+            dma((nb_a, 2)), dma((max(chips - 1, 1), 2 * nb_a)), dma((max(chips - 1, 1), 2 * nb_a)),
+            dma((1,)), dma((1,)),
+            dma((nb_a,)), dma((nb_a,)), dma((nb_a,)), dma((nb_t,)),
+            dma((2,)), dma((T + 1, nb_t, np_)),
             pltpu.SemaphoreType.REGULAR((2,)),
         ],
         compiler_params=pltpu.CompilerParams(

time: 75.7 us -> 74.9 us (0.989)
  Pallas kernels: 73.8 us -> 72.8 us
    pallas_call x1, Pallas kernels: 73.8 us -> 72.8 us  [on_device(): pl.pallas_call(functools.partial(kernel, A, T), out_shape=pltpu.VMEM((row...]
where the time goes in v5:
time: 74.9 us; the launch traced here: 73.7 us
  Pallas kernels  72.8 us (97%)
  local copies, waits for them, and re-layouts  0.97 us (1%)
    pallas_call x1, Pallas kernels, on_device(): pl.pallas_call(functools.partial(kernel, A, T), out_shape=pltpu.VMEM((row...  72.8 us

profile of v5, /device:TPU:16, one launch (start us, length us, event | category | flops | bytes accessed | tf_op | source)
XLA Modules:
  0.0 73.7 jit_solution(12758860367698721432)
XLA Ops:
  0.0 72.8 %shard_map.73 = bf16[256,2048]{1,0:T(8,128)(2,1)S(1)} custom-call(s32[8]{0:T(128)} %ids_hbm.1, s32[8]{0:T(128)} %live_hbm.1, s32[128]{0:T(128)} %slots_hbm.1, bf16[256,2048]{1,0:T(8,128)(2,1)} %tok_hbm.1, bf16[2048,2048]{1,0:T(8,128)(2,1)} %w_hbm.1, bf16[32,16,2048]{2,1,0:T(8,128)(2,1)} %dn_hbm.1, bf16[32,16,8192]{2,1,0:T(8,128)(2,1)} %up_hbm.1), custom_call_target="tpu_custom_call" | custom-call | tf_op jit(solution)/shard_map/pallas_call | solution.py:571
  72.8 1.0 %copy.9 = bf16[256,2048]{1,0:T(8,128)(2,1)} copy(bf16[256,2048]{1,0:T(8,128)(2,1)S(1)} %shard_map.73) | data formatting | bytes 2097152

commit v6 on v5

--- a/solution.py
+++ b/solution.py
@@ -120,20 +120,16 @@
         w_load(p).wait()
         buf[pre_way, pre_slot, 0, p] = base(a * nb_a, p).astype(buf.dtype)
 
+    for p in range(1, min(2, np_)):
+        w_load(p).start()
     tok_load(0).wait()
     for b in range(1, nb_a):
         tok_load(b).start()
-    for p in range(1, min(2, np_)):
-        w_load(p).start()
-
     if near:
         @pl.when(pre)
         def _():
             for p in range(early):
                 lead_unit(p)
-
-    for p in range(2, np_):
-        w_load(p).start()
 
     ends = jnp.where(t > 0, 1, 0) + jnp.where(t < T - 1, 1, 0)
     pl.semaphore_wait(barrier, A - 1 + ends)
@@ -237,17 +233,15 @@
 
     if near:
         lead_units(early, min(early + 1, np_))
+    for p in range(2, np_):
+        w_load(p).start()
     from_partner(0)
     if near:
         lead_units(min(early + 1, np_), np_)
-    dn_load.start()
-    up_load.start()
     tables = [
         pltpu.make_async_copy(src, dst, sm_sem.at[i])
         for i, (src, dst) in enumerate(((ids_hbm, ids), (live_hbm, live), (slots_hbm, slots)))
     ]
-    for c in tables:
-        c.start()
     if not near:
         rest_from_partner()
 
@@ -456,6 +450,8 @@
 
         @pl.when(n == min(1, steps - 1) * np_)
         def _():
+            for c in tables + [dn_load, up_load]:
+                c.start()
             relay()
 
         @pl.when(n == min(2, steps - 1) * np_)

time: 74.9 us -> 74.6 us (level)
  no operation moved by 1% of the time
where the time goes in v6:
time: 74.6 us; the launch traced here: 73.7 us
  Pallas kernels  72.8 us (98%)
  local copies, waits for them, and re-layouts  0.97 us (1%)
    pallas_call x1, Pallas kernels, on_device(): pl.pallas_call(functools.partial(kernel, A, T), out_shape=pltpu.VMEM((row...  72.8 us

profile of v6, /device:TPU:16, one launch (start us, length us, event | category | flops | bytes accessed | tf_op | source)
XLA Modules:
  0.0 73.7 jit_solution(16638611255745260426)
XLA Ops:
  0.0 72.8 %shard_map.73 = bf16[256,2048]{1,0:T(8,128)(2,1)S(1)} custom-call(s32[8]{0:T(128)} %ids_hbm.1, s32[8]{0:T(128)} %live_hbm.1, s32[128]{0:T(128)} %slots_hbm.1, bf16[256,2048]{1,0:T(8,128)(2,1)} %tok_hbm.1, bf16[2048,2048]{1,0:T(8,128)(2,1)} %w_hbm.1, bf16[32,16,2048]{2,1,0:T(8,128)(2,1)} %dn_hbm.1, bf16[32,16,8192]{2,1,0:T(8,128)(2,1)} %up_hbm.1), custom_call_target="tpu_custom_call" | custom-call | tf_op jit(solution)/shard_map/pallas_call | solution.py:567
  72.8 1.0 %copy.9 = bf16[256,2048]{1,0:T(8,128)(2,1)} copy(bf16[256,2048]{1,0:T(8,128)(2,1)S(1)} %shard_map.73) | data formatting | bytes 2097152

commit v7 on v6

--- a/solution.py
+++ b/solution.py
@@ -10,7 +10,6 @@
 BLOCK = 128
 SCALE = 2.0
 MESH = pl.DeviceIdType.MESH
-PRE = 1
 LAG = 3
 
 
@@ -41,6 +40,15 @@
             tok_hbm.at[pl.ds(b * BLOCK, BLOCK)], tok.at[a * nb_a + b], ld_sem.at[b]
         )
 
+    piece = cp // 2 if cp % 256 == 0 else cp
+    pieces = cp // piece
+
+    def w_piece(i):
+        c = pl.ds(i * piece, piece)
+        return pltpu.make_async_copy(
+            w_hbm.at[:, c], w.at[0, :, c], w_sem.at[np_ if i else 0]
+        )
+
     def w_load(p):
         c = pl.ds(pl.multiple_of(p * cp, cp), cp)
         return pltpu.make_async_copy(w_hbm.at[:, c], w.at[p], w_sem.at[p])
@@ -49,7 +57,7 @@
     up_load = pltpu.make_async_copy(up_hbm, up, ld_sem.at[1])
 
     tok_load(0).start()
-    w_load(0).start()
+    w_piece(0).start()
 
     barrier = pltpu.get_barrier_semaphore()
 
@@ -110,7 +118,6 @@
     def base(q, p):
         return jnp.dot(tok[q], w[p], preferred_element_type=jnp.float32)
 
-    early = min(PRE, np_)
     if near:
         pre_way = jnp.where(t == 0, 0, 1)
         pre_slot = jnp.where(t == 0, jnp.maximum(a - 1, 0), jnp.minimum(a, T - 2))
@@ -120,16 +127,39 @@
         w_load(p).wait()
         buf[pre_way, pre_slot, 0, p] = base(a * nb_a, p).astype(buf.dtype)
 
+    def lead_piece(i):
+        w_piece(i).wait()
+        c = slice(i * piece, (i + 1) * piece)
+        buf[pre_way, pre_slot, 0, 0, :, c] = jnp.dot(
+            tok[a * nb_a], w[0, :, c], preferred_element_type=jnp.float32
+        ).astype(buf.dtype)
+
+    def send_piece(i):
+        r = buf.at[pre_way, pre_slot, 0, 0, :, pl.ds(i * piece, piece)]
+        pltpu.make_async_remote_copy(
+            r, r, fl_ss.at[pre_way], fl_rs.at[row(pre_way, pre_to, pre_slot), 0, 0],
+            device_id={"tensor": pre_to}, device_id_type=MESH,
+        ).start()
+
+    for i in range(1, pieces):
+        w_piece(i).start()
+    for b in range(1, nb_a):
+        tok_load(b).start()
     for p in range(1, min(2, np_)):
         w_load(p).start()
     tok_load(0).wait()
-    for b in range(1, nb_a):
-        tok_load(b).start()
     if near:
         @pl.when(pre)
         def _():
-            for p in range(early):
-                lead_unit(p)
+            lead_piece(0)
+
+        @pl.when(jnp.logical_and(pre, t == 0))
+        def _():
+            for i in range(1, pieces):
+                lead_piece(i)
+
+    for p in range(2, np_):
+        w_load(p).start()
 
     ends = jnp.where(t > 0, 1, 0) + jnp.where(t < T - 1, 1, 0)
     pl.semaphore_wait(barrier, A - 1 + ends)
@@ -183,8 +213,12 @@
 
         @pl.when(pre)
         def _():
-            for p in range(early):
-                flow(pre_way, pre_to, pre_slot, 0, p).start()
+            send_piece(0)
+
+        @pl.when(jnp.logical_and(pre, t == 0))
+        def _():
+            for i in range(1, pieces):
+                send_piece(i)
 
     for b in range(nb_a):
         if b:
@@ -232,12 +266,16 @@
                 send_x(m)
 
     if near:
-        lead_units(early, min(early + 1, np_))
-    for p in range(2, np_):
-        w_load(p).start()
+        @pl.when(jnp.logical_and(pre, t > 0))
+        def _():
+            for i in range(1, pieces):
+                lead_piece(i)
+                send_piece(i)
+
+        lead_units(1, min(2, np_))
     from_partner(0)
     if near:
-        lead_units(min(early + 1, np_), np_)
+        lead_units(min(2, np_), np_)
     tables = [
         pltpu.make_async_copy(src, dst, sm_sem.at[i])
         for i, (src, dst) in enumerate(((ids_hbm, ids), (live_hbm, live), (slots_hbm, slots)))
@@ -468,7 +506,14 @@
 
         @pl.when(loaded)
         def _():
-            w_load(p).wait()
+            @pl.when(p == 0)
+            def _():
+                for i in range(pieces):
+                    w_piece(i).wait()
+
+            @pl.when(p > 0)
+            def _():
+                w_load(p).wait()
 
         advance(0, n)
         advance(1, n)
@@ -586,7 +631,7 @@
             pltpu.VMEM((nb_a, rank, BLOCK), bf),
             pltpu.VMEM((nb_a, T, rank, BLOCK), bf),
             pltpu.VMEM((nb_t, T, rank, BLOCK), bf),
-            dma((3,)), dma((max(nb_a, 2),)), dma((np_,)), dma((5,)),
+            dma((3,)), dma((max(nb_a, 2),)), dma((np_ + 1,)), dma((5,)),
             dma((nb_a, 2)), dma((max(chips - 1, 1), 2 * nb_a)), dma((max(chips - 1, 1), 2 * nb_a)),
             dma((1,)), dma((1,)),
             dma((nb_a,)), dma((nb_a,)), dma((nb_a,)), dma((nb_t,)),

time: 74.6 us -> 74.2 us (level)
  no operation moved by 1% of the time
where the time goes in v7:
time: 74.2 us; the launch traced here: 73.4 us
  Pallas kernels  72.4 us (98%)
  local copies, waits for them, and re-layouts  0.97 us (1%)
    pallas_call x1, Pallas kernels, on_device(): pl.pallas_call(functools.partial(kernel, A, T), out_shape=pltpu.VMEM((row...  72.4 us

profile of v7, /device:TPU:16, one launch (start us, length us, event | category | flops | bytes accessed | tf_op | source)
XLA Modules:
  0.0 73.4 jit_solution(11701348402738557109)
XLA Ops:
  0.0 72.4 %shard_map.73 = bf16[256,2048]{1,0:T(8,128)(2,1)S(1)} custom-call(s32[8]{0:T(128)} %ids_hbm.1, s32[8]{0:T(128)} %live_hbm.1, s32[128]{0:T(128)} %slots_hbm.1, bf16[256,2048]{1,0:T(8,128)(2,1)} %tok_hbm.1, bf16[2048,2048]{1,0:T(8,128)(2,1)} %w_hbm.1, bf16[32,16,2048]{2,1,0:T(8,128)(2,1)} %dn_hbm.1, bf16[32,16,8192]{2,1,0:T(8,128)(2,1)} %up_hbm.1), custom_call_target="tpu_custom_call" | custom-call | tf_op jit(solution)/shard_map/pallas_call | solution.py:612
  72.4 1.0 %copy.9 = bf16[256,2048]{1,0:T(8,128)(2,1)} copy(bf16[256,2048]{1,0:T(8,128)(2,1)S(1)} %shard_map.73) | data formatting | bytes 2097152

commit v8 on v7

--- a/solution.py
+++ b/solution.py
@@ -10,7 +10,8 @@
 BLOCK = 128
 SCALE = 2.0
 MESH = pl.DeviceIdType.MESH
-LAG = 3
+LAG = 4
+GROUP = 2
 
 
 def kernel(
@@ -32,6 +33,7 @@
     per_dev = dn_hbm.shape[0]
     np_, _, cp = w.shape
     cols = np_ * cp
+    group = GROUP if np_ % GROUP == 0 else 1
     steps = (T - 1) * nb_t
     near = chips == 2 and nb_a == nb_t
 
@@ -99,7 +101,7 @@
     def flow(way, to, slot, h, p):
         return pltpu.make_async_remote_copy(
             buf.at[way, slot, h, p], buf.at[way, slot, h, p],
-            fl_ss.at[way], fl_rs.at[row(way, to, slot), h, p],
+            fl_ss.at[way], fl_rs.at[row(way, to, slot), h, p // group],
             device_id={"tensor": to}, device_id_type=MESH,
         )
 
@@ -109,9 +111,9 @@
         return flow(way, left if way else right, slot, h, p)
 
     def arrival(way, slot, h, p):
-        return pltpu.make_async_remote_copy(
-            buf.at[way, slot, h, p], buf.at[way, slot, h, p],
-            fl_ss.at[way], fl_rs.at[row(way, t, slot), h, p],
+        r = buf.at[way, slot, h, pl.ds(p, group)]
+        return pltpu.make_async_remote_copy(
+            r, r, fl_ss.at[way], fl_rs.at[row(way, t, slot), h, p // group],
             device_id={"tensor": left if way else right}, device_id_type=MESH,
         )
 
@@ -461,7 +463,10 @@
 
             @pl.when(jnp.logical_not(fresh))
             def _():
-                arrival(way, slot, h, p).wait_recv()
+                @pl.when(p % group == 0)
+                def _():
+                    arrival(way, slot, h, p).wait_recv()
+
                 buf[way, slot, h, p] = (
                     mine + buf[way, slot, h, p].astype(jnp.float32)
                 ).astype(buf.dtype)
@@ -550,7 +555,7 @@
         def _():
             col_copy(b).wait_send()
 
-    def last(n, _):
+    def adapters(n, _):
         h, p = n // np_, n % np_
         own = lax.div(slot_of(t * nb_t + h), per_dev)
         u = up_recv[own, h, :, pl.ds(pl.multiple_of(p * cp, cp), cp)]
@@ -560,16 +565,29 @@
             preferred_element_type=jnp.float32,
         )
 
+        return 0
+
+    lax.fori_loop(0, nb_t * np_, adapters, 0)
+
+    def last(n, _):
+        h, p = n // np_, n % np_
+
         @pl.when(t > 0)
         def _():
             slot = jnp.maximum(t - 1, 0)
-            arrival(0, slot, h, p).wait_recv()
+            @pl.when(p % group == 0)
+            def _():
+                arrival(0, slot, h, p).wait_recv()
+
             acc[h, p] = acc[h, p] + buf[0, slot, h, p].astype(jnp.float32)
 
         @pl.when(t < T - 1)
         def _():
             slot = jnp.minimum(t, T - 2)
-            arrival(1, slot, h, p).wait_recv()
+            @pl.when(p % group == 0)
+            def _():
+                arrival(1, slot, h, p).wait_recv()
+
             acc[h, p] = acc[h, p] + buf[1, slot, h, p].astype(jnp.float32)
 
         out_ref[
@@ -635,7 +653,7 @@
             dma((nb_a, 2)), dma((max(chips - 1, 1), 2 * nb_a)), dma((max(chips - 1, 1), 2 * nb_a)),
             dma((1,)), dma((1,)),
             dma((nb_a,)), dma((nb_a,)), dma((nb_a,)), dma((nb_t,)),
-            dma((2,)), dma((T + 1, nb_t, np_)),
+            dma((2,)), dma((T + 1, nb_t, np_ // GROUP if np_ % GROUP == 0 else np_)),
             pltpu.SemaphoreType.REGULAR((2,)),
         ],
         compiler_params=pltpu.CompilerParams(

time: 74.2 us -> 74.1 us (level)
  no operation moved by 1% of the time
where the time goes in v8:
time: 74.1 us; the launch traced here: 73.3 us
  Pallas kernels  72.3 us (98%)
  local copies, waits for them, and re-layouts  0.97 us (1%)
    pallas_call x1, Pallas kernels, on_device(): pl.pallas_call(functools.partial(kernel, A, T), out_shape=pltpu.VMEM((row...  72.3 us

profile of v8, /device:TPU:16, one launch (start us, length us, event | category | flops | bytes accessed | tf_op | source)
XLA Modules:
  0.0 73.3 jit_solution(11351048794753802258)
XLA Ops:
  0.0 72.3 %shard_map.73 = bf16[256,2048]{1,0:T(8,128)(2,1)S(1)} custom-call(s32[8]{0:T(128)} %ids_hbm.1, s32[8]{0:T(128)} %live_hbm.1, s32[128]{0:T(128)} %slots_hbm.1, bf16[256,2048]{1,0:T(8,128)(2,1)} %tok_hbm.1, bf16[2048,2048]{1,0:T(8,128)(2,1)} %w_hbm.1, bf16[32,16,2048]{2,1,0:T(8,128)(2,1)} %dn_hbm.1, bf16[32,16,8192]{2,1,0:T(8,128)(2,1)} %up_hbm.1), custom_call_target="tpu_custom_call" | custom-call | tf_op jit(solution)/shard_map/pallas_call | solution.py:630
  72.3 1.0 %copy.9 = bf16[256,2048]{1,0:T(8,128)(2,1)} copy(bf16[256,2048]{1,0:T(8,128)(2,1)S(1)} %shard_map.73) | data formatting | bytes 2097152

commit v9 on v8

--- a/solution.py
+++ b/solution.py
@@ -10,8 +10,8 @@
 BLOCK = 128
 SCALE = 2.0
 MESH = pl.DeviceIdType.MESH
-LAG = 4
-GROUP = 2
+LAG = 6
+GROUP = 4
 
 
 def kernel(

time: 74.1 us -> 76.4 us (1.031)
  the two profiles are of different devices: /device:TPU:16 before, /device:TPU:11 now
where the time goes in v9:
time: 76.4 us; the launch traced here: 76.2 us
  Pallas kernels  75.3 us (99%)
  local copies, waits for them, and re-layouts  0.97 us (1%)
    pallas_call x1, Pallas kernels, on_device(): pl.pallas_call(functools.partial(kernel, A, T), out_shape=pltpu.VMEM((row...  75.3 us

profile of v9, /device:TPU:11, one launch (start us, length us, event | category | flops | bytes accessed | tf_op | source)
XLA Modules:
  0.0 76.2 jit_solution(11146090641097443007)
XLA Ops:
  0.0 75.3 %shard_map.73 = bf16[256,2048]{1,0:T(8,128)(2,1)S(1)} custom-call(s32[8]{0:T(128)} %ids_hbm.1, s32[8]{0:T(128)} %live_hbm.1, s32[128]{0:T(128)} %slots_hbm.1, bf16[256,2048]{1,0:T(8,128)(2,1)} %tok_hbm.1, bf16[2048,2048]{1,0:T(8,128)(2,1)} %w_hbm.1, bf16[32,16,2048]{2,1,0:T(8,128)(2,1)} %dn_hbm.1, bf16[32,16,8192]{2,1,0:T(8,128)(2,1)} %up_hbm.1), custom_call_target="tpu_custom_call" | custom-call | tf_op jit(solution)/shard_map/pallas_call | solution.py:630
  75.3 1.0 %copy.9 = bf16[256,2048]{1,0:T(8,128)(2,1)} copy(bf16[256,2048]{1,0:T(8,128)(2,1)S(1)} %shard_map.73) | data formatting | bytes 2097152
